TPU v7x, 32 devices: a whole 2x2x4 slice. The times are simulated.
32 devices in a mesh: row: 8 (over z, core), col: 4 (over y, x).
Axes of the slice: x: 2, y: 2, z: 4, core: 2. Of those that a mesh axis runs over, the one named last changes fastest.
Arguments:
- ancestor_inverse: float32 [12288, 12288], P('row', 'col'), may hold values from -6 to 6
- panel: float32 [5632, 512], P('col', 'row'), may hold values from -0.078125 to 0.078125
- unit_inverse: float32 [512, 512], P('row'), may hold values from -1 to 1, as said below
- pivot_inverse: float32 [512, 512], P('row', 'col'), may hold values from -6 to 6
- panel_blocks: int32 [44], replicated, may hold values from 0 to 95, as said below
Outputs:
- inverse_row: float32 [512, 12288], P('col', 'row')
- diagonal_block: float32 [512, 512], P('row', 'col')
Inputs may be any that keep to these rules, and one draw needn't show every extreme that they name: `panel_blocks`: Distinct, in no particular order. Among the window blocks c * 24 to c * 24 + 23 of any process column c at most 12 are listed, and exactly 12 for some columns. `unit_inverse`: unit lower triangular: ones on the diagonal, zeros above it.
All inputs are finite; a program needn't handle non-finite values.
Results may differ from a plain program's by a relative error of at most 0.00011.
Values sent between devices are 32-bit elements; how exact they have to be, the bound alone decides.
A program may use at most 128 MiB of HBM per device.

v0:
```python
import jax
import jax.numpy as jnp
from jax import lax
from jax.sharding import PartitionSpec as P

BLK = 128


def broadcast(value, axis, root):
    mine = lax.axis_index(axis) == root
    return lax.psum(jnp.where(mine, value, jnp.zeros_like(value)), axis)


def place_blocks(stacked, block_ids, wanted):
    onehot = (block_ids[None, :] == wanted[:, None]).astype(jnp.float32)
    placed = jnp.einsum("kp,pbw->kbw", onehot, stacked, precision=lax.Precision.HIGHEST)
    return placed.reshape(wanted.shape[0] * stacked.shape[1], stacked.shape[2])


def on_device(ancestor_inverse, panel, unit_inverse, pivot_inverse, panel_blocks):
    highest = lax.Precision.HIGHEST
    row_index = lax.axis_index("row")
    col_index = lax.axis_index("col")
    rows_here, cols_here = ancestor_inverse.shape
    width = unit_inverse.shape[1]
    block_total = panel_blocks.shape[0]
    range_blocks = cols_here // BLK
    row_blocks = rows_here // BLK
    first_block = col_index * range_blocks
    partial_value = jnp.dot(
        panel, unit_inverse, precision=highest, preferred_element_type=jnp.float32
    )
    normal = lax.psum_scatter(partial_value, "row", scatter_dimension=1, tiled=True)
    all_rows = lax.all_gather(normal, "col", axis=0, tiled=True)
    stacked = all_rows.reshape(block_total, BLK, all_rows.shape[1])
    slot_count = range_blocks // 2
    in_range = ((panel_blocks >= first_block) & (panel_blocks < first_block + range_blocks)).astype(
        jnp.int32
    )
    rank_of = jnp.cumsum(in_range) - 1
    slot_ids = jnp.arange(slot_count, dtype=jnp.int32)
    selected = (in_range[None, :] == 1) & (rank_of[None, :] == slot_ids[:, None])
    chosen = jnp.einsum("sp,pbw->sbw", selected.astype(jnp.float32), stacked, precision=highest)
    chosen = chosen.reshape(slot_count * BLK, stacked.shape[2])
    chosen_ids = jnp.sum(jnp.where(selected, panel_blocks[None, :], 0), axis=1)
    slot_live = jnp.sum(selected.astype(jnp.int32), axis=1) > 0
    window_ids = jnp.where(slot_live, chosen_ids, -1)
    local_ids = jnp.clip(chosen_ids - first_block, 0, range_blocks - 1)
    window = lax.all_gather(chosen, "row", axis=1, tiled=True)
    columns = jnp.take(ancestor_inverse.reshape(rows_here, range_blocks, BLK), local_ids, axis=1)
    columns = columns.reshape(rows_here, slot_count * BLK)
    inverse_tile = lax.psum_scatter(
        -lax.dot_general(
            window,
            columns,
            (((0,), (1,)), ((), ())),
            precision=highest,
            preferred_element_type=jnp.float32,
        ),
        "col",
        scatter_dimension=0,
        tiled=True,
    )
    row_ids = row_index * row_blocks + jnp.arange(row_blocks, dtype=jnp.int32)
    window_stack = window.reshape(window.shape[0] // BLK, BLK, width)
    candidate = place_blocks(window_stack, window_ids, row_ids)
    owner = row_index * rows_here // cols_here
    own_window = broadcast(candidate, "col", owner)
    crossed = -lax.dot_general(
        own_window,
        inverse_tile,
        (((0,), (1,)), ((), ())),
        precision=highest,
        preferred_element_type=jnp.float32,
    )
    diagonal_block = pivot_inverse + lax.psum_scatter(
        crossed, "row", scatter_dimension=0, tiled=True
    )
    return (inverse_tile, diagonal_block)


def solution(mesh):
    return jax.shard_map(
        on_device,
        mesh=mesh,
        in_specs=(P("row", "col"), P("col", "row"), P("row", None), P("row", "col"), P()),
        out_specs=(P("col", "row"), P("row", "col")),
        check_vma=False,
    )
```

profile of v0, /device:TPU:0, one launch (start us, length us, event | category | flops | bytes accessed | tf_op | source)
XLA Modules:
  0.0 318.0 jit_solution(3767256040483934672)
XLA Ops:
  7.2 0.0 copy-start
  7.2 0.0 copy-start.4
  7.2 0.0 reduce-scatter.4.cloned.1.call-start
  7.2 0.9 copy-done
  8.2 4.9 %fusion.16 = f32[1408,512]{0,1:T(8,128)} fusion(f32[1408,64]{0,1:T(8,128)S(1)} %copy-done, f32[64,512]{1,0:T(8,128)} %param.7), kind=kOutput, calls=%fused_computation.32 | convolution fusion | flops 553648128 | bytes 3375104 | tf_op jit(solution)/shard_map/dot_general | solution.py:30
  13.1 0.0 reduce-scatter.4.cloned.1.call-update
  13.1 0.0 all-gather.3.cloned.1.call-start
  13.2 41.8 %reduce-scatter.4.cloned.1.call-done = f32[1408,64]{0,1:T(8,128)} async-done(((f32[1408,512]{0,1:T(8,128)}), f32[1408,64]{0,1:T(8,128)}) %reduce-scatter.4.cloned.1.call-update) | async-done | bytes 360464 | tf_op jit(solution)/shard_map/reduce_scatter | solution.py:33
  54.9 0.0 all-gather.3.cloned.1.call-update
  55.0 0.0 all-gather.5.cloned.1.call-start
  55.0 0.0 copy-done.4
  55.0 0.1 copy.13
  55.1 0.1 reduce-window.8
  55.2 0.1 add_reduce_fusion
  55.3 30.5 %all-gather.3.cloned.1.call-done = f32[5632,64]{0,1:T(8,128)} async-done(((f32[1408,64]{0,1:T(8,128)}), f32[5632,64]{0,1:T(8,128)}) %all-gather.3.cloned.1.call-update) | async-done | bytes 1441808 | tf_op jit(solution)/shard_map/all_gather | solution.py:34
  85.8 1.5 reshape.93
  87.3 0.6 fusion.7
  87.9 0.9 copy.26
  88.8 0.0 all-gather.5.cloned.1.call-update
  88.8 0.0 all-reduce.2.cloned.1.call-start
  88.9 18.8 %copy.14 = f32[1536,3072]{0,1:T(8,128)} copy(f32[1536,3072]{1,0:T(8,128)} %param.5) | data formatting | bytes 37748736 | tf_op args[0]
  107.7 18.7 %copy.15 = f32[1536,24,128]{2,0,1:T(8,128)} copy(f32[1536,24,128]{0,2,1:T(8,128)} %bitcast.34) | data formatting | bytes 37748736 | tf_op jit(solution)/shard_map/reshape | solution.py:50
  126.4 0.1 convert_reduce_fusion
  126.5 0.6 all-gather.5.cloned.1.call-done
  127.2 2.4 copy.17
  129.6 4.0 %fusion.2 = f32[12,128,512]{2,0,1:T(8,128)S(1)} fusion(f32[12,128,512]{2,1,0:T(8,128)S(1)} %bitcast.36, pred[]{:T(512)S(6)} %eq.41, s32[12]{0:T(128)S(1)} %get-tuple-element.6, s32[12]{0:T(128)S(1)} %get-tuple-element.7), kind=kOutput, calls=%fused_computation.5 | convolution fusion | flops 114032784 | bytes 6291553 | tf_op jit(solution)/shard_map/kp,pbw->kbw/dot_general | solution.py:16
  133.6 3.5 %copy.19 = f32[12,128,512]{2,1,0:T(8,128)} copy(f32[12,128,512]{2,0,1:T(8,128)S(1)} %fusion.2) | data formatting | bytes 6291456 | tf_op jit(solution)/shard_map/jit(_where)/select_n | solution.py:11
  137.1 0.0 all-reduce.2.cloned.1.call-update
  137.1 0.0 reduce-scatter.6.cloned.1.call-start
  137.2 12.3 %gather_fusion = f32[12,1536,128]{2,1,0:T(8,128)} fusion(f32[1536,24,128]{2,0,1:T(8,128)} %copy.15, s32[1024]{0:T(1024)S(1)} %pad_clamp_fusion), kind=kCustom, calls=%fused_computation | custom fusion | bytes 18874416 | tf_op jit(solution)/shard_map/jit(_take)/gather | solution.py:50
  149.5 9.8 %copy.16 = f32[1536,12,128]{0,2,1:T(8,128)} copy(f32[1536,12,128]{2,0,1:T(8,128)} %bitcast.35) | data formatting | bytes 18874368 | tf_op jit(solution)/shard_map/jit(_take)/gather | solution.py:50
  159.2 0.1 broadcast_bitcast_fusion
  159.3 0.0 copy-start.2
  159.3 4.6 %bitcast_select_fusion = f32[1536,1536]{0,1:T(8,128)S(1)} fusion(f32[1536,12,128]{0,2,1:T(8,128)} %copy.16, pred[1536]{0:T(1024)(128)(4,1)S(1)} %broadcast_bitcast_fusion), kind=kLoop, calls=%fused_computation.1 | loop fusion | flops 2359296 | bytes 18875904 | tf_op jit(solution)/shard_map/jit(_take)/select_n | solution.py:50
  164.0 0.1 copy-done.2
  164.0 17.1 %convolution_negate_fusion = f32[512,1536]{1,0:T(8,128)} fusion(f32[1536,512]{0,1:T(8,128)S(1)} %copy-done.2, f32[1536,1536]{0,1:T(8,128)S(1)} %bitcast_select_fusion), kind=kOutput, calls=%fused_computation.4 | convolution fusion | flops 14496301056 | bytes 15728640 | tf_op jit(solution)/shard_map/dot_general | solution.py:53
  181.1 0.0 copy-start.1
  181.1 0.0 copy-start.3
  181.1 0.0 reduce-scatter.6.cloned.1.call-update
  181.1 0.0 reduce-scatter.8.cloned.1.call-start
  181.2 42.4 %all-reduce.2.cloned.1.call-done = f32[1536,512]{1,0:T(8,128)} async-done(((f32[1536,512]{1,0:T(8,128)}), f32[1536,512]{1,0:T(8,128)}) %all-reduce.2.cloned.1.call-update) | async-done | bytes 3145744 | tf_op jit(solution)/shard_map/psum | solution.py:11
  223.6 47.3 %reduce-scatter.6.cloned.1.call-done = f32[128,1536]{1,0:T(8,128)} async-done(((f32[512,1536]{1,0:T(8,128)}), f32[128,1536]{1,0:T(8,128)}) %reduce-scatter.6.cloned.1.call-update) | async-done | bytes 786448 | tf_op jit(solution)/shard_map/reduce_scatter | solution.py:52
  270.9 7.8 %convolution_negate_fusion.1 = f32[512,128]{1,0:T(8,128)} fusion(f32[1536,512]{1,0:T(8,128)} %all-reduce.2.cloned.1.call-done, f32[128,1536]{1,0:T(8,128)} %reduce-scatter.6.cloned.1.call-done), kind=kOutput, calls=%fused_computation.6 | convolution fusion | flops 1208025088 | bytes 4194304 | tf_op jit(solution)/shard_map/dot_general | solution.py:69
  278.8 0.0 reduce-scatter.8.cloned.1.call-update
  278.8 31.0 %reduce-scatter.8.cloned.1.call-done = f32[64,128]{1,0:T(8,128)} async-done(((f32[512,128]{1,0:T(8,128)}), f32[64,128]{1,0:T(8,128)}) %reduce-scatter.8.cloned.1.call-update) | async-done | bytes 32784 | tf_op jit(solution)/shard_map/reduce_scatter | solution.py:76
  309.8 0.0 copy-done.3
  309.8 1.4 add.51
  311.1 0.0 copy-done.1
  (5 shorter events, 0.0 us)
Async XLA Ops:
  7.2 1.0 copy-start
  7.2 47.8 %copy-start.4 = (s32[44]{0:T(128)S(1)}, s32[44]{0:T(128)}, u32[]{:S(2)}) copy-start(s32[44]{0:T(128)} %param.9) | copy-start | bytes 532
  7.2 47.8 %reduce-scatter.4.cloned.1.call-start = ((), (), s32[]{:S(2)}) async-start(), calls=%async_computation.3 | async-start | bytes 3244032 | tf_op jit(solution)/shard_map/reduce_scatter | solution.py:33
  13.1 72.7 %all-gather.3.cloned.1.call-start = ((), (), s32[]{:S(2)}) async-start(), calls=%async_computation.4 | async-start | bytes 1802240 | tf_op jit(solution)/shard_map/all_gather | solution.py:34
  55.0 72.2 %all-gather.5.cloned.1.call-start = ((), (), s32[]{:S(2)}) async-start(), calls=%async_computation.5 | async-start | bytes 3538944 | tf_op jit(solution)/shard_map/all_gather | solution.py:49
  88.8 134.8 %all-reduce.2.cloned.1.call-start = ((), (), s32[]{:S(2)}) async-start(), calls=%async_computation.7 | async-start | bytes 6291456 | tf_op jit(solution)/shard_map/psum | solution.py:11
  137.1 133.8 %reduce-scatter.6.cloned.1.call-start = ((), (), s32[]{:S(2)}) async-start(), calls=%async_computation.6 | async-start | bytes 3932160 | tf_op jit(solution)/shard_map/reduce_scatter | solution.py:52
  159.3 4.7 %copy-start.2 = (f32[1536,512]{0,1:T(8,128)S(1)}, f32[1536,512]{0,1:T(8,128)}, u32[]{:S(2)}) copy-start(f32[1536,512]{0,1:T(8,128)} %all-gather.5.cloned.1.call-done) | copy-start | bytes 9437188
  181.1 130.0 %copy-start.1 = (f32[1408,64]{0,1:T(8,128)S(1)}, f32[1408,64]{0,1:T(8,128)}, u32[]{:S(2)}) copy-start(f32[1408,64]{0,1:T(8,128)} %param.6) | copy-start | bytes 1081348
  181.1 128.7 %copy-start.3 = (f32[64,128]{1,0:T(8,128)S(1)}, f32[64,128]{1,0:T(8,128)}, u32[]{:S(2)}) copy-start(f32[64,128]{1,0:T(8,128)} %param.8) | copy-start | bytes 98308
  181.1 128.6 %reduce-scatter.8.cloned.1.call-start = ((), (), s32[]{:S(2)}) async-start(), calls=%async_computation.8 | async-start | bytes 294912 | tf_op jit(solution)/shard_map/reduce_scatter | solution.py:76
Sparse Core Ops, SparseCore 0:
  13.2 41.6 reduce-scatter.3
  56.8 28.9 all-gather.2
  88.9 38.2 all-gather.4
  137.2 86.3 all-reduce.1
  227.0 43.8 reduce-scatter.5
  278.9 30.8 reduce-scatter.7
where the time goes:
time: 319 us; the launch traced here: 318 us
  waiting for transfers between devices  194 us (61%)
  local copies, waits for them, and re-layouts  68.9 us (22%)
  matrix products  34.5 us (11%)
  between operations  14.2 us (4%)
  other arithmetic  6.36 us (2%)
    reduce_scatter x1, waiting for transfers between devices, on_device(): lax.psum_scatter(-lax.dot_general(window, columns, (((0,), (1,)), ((), ()...  47.3 us
    psum x1, waiting for transfers between devices, broadcast(): return lax.psum(jnp.where(mine, value, jnp.zeros_like(value)), axis)  42.4 us
    reduce_scatter x1, waiting for transfers between devices, on_device(): lax.psum_scatter(partial_value, 'row', scatter_dimension=1, tiled=True)  41.8 us
    reduce_scatter x1, waiting for transfers between devices, on_device(): lax.psum_scatter(crossed, 'row', scatter_dimension=0, tiled=True)  31 us
    all_gather x1, waiting for transfers between devices, on_device(): all_rows = lax.all_gather(normal, 'col', axis=0, tiled=True)  30.5 us
    gather x2, local copies, waits for them, and re-layouts, on_device(): jnp.take(ancestor_inverse.reshape(rows_here, range_blocks, BLK), local_id...  22 us
    unnamed x12, local copies, waits for them, and re-layouts  20.7 us
    reshape x1, local copies, waits for them, and re-layouts, on_device(): ancestor_inverse.reshape(rows_here, range_blocks, BLK)  18.7 us
  transfers between devices with their start and end apart: 6, of which 6 were waited for; matrix products, arithmetic and copies ran while one was open for 26% of the time, Pallas kernels for 0%

commit v1 on v0

--- a/solution.py
+++ b/solution.py
@@ -8,7 +8,8 @@
 
 def broadcast(value, axis, root):
     mine = lax.axis_index(axis) == root
-    return lax.psum(jnp.where(mine, value, jnp.zeros_like(value)), axis)
+    units_run = lambda packet, axis_key: lax.all_gather(packet, axis_key).sum(axis=0)
+    return units_run(jnp.where(mine, value, jnp.zeros_like(value)), axis)
 
 
 def place_blocks(stacked, block_ids, wanted):

time: 319 us -> 353 us (1.11)
  waiting for transfers between devices: 194 us -> 223 us
  other arithmetic: 6.36 us -> 12.8 us
    psum x1 -> x0, waiting for transfers between devices: 42.4 us -> none  [broadcast(): return lax.psum(jnp.where(mine, value, jnp.zeros_like(value)), axis)]
    all_gather x0 -> x1, waiting for transfers between devices: none -> 40.5 us  [broadcast(): lax.all_gather(packet, axis_key).sum(axis=0)]
    all_gather x1, waiting for transfers between devices: 0.65 us -> 38.2 us  [on_device(): window = lax.all_gather(chosen, 'row', axis=1, tiled=True)]
    reduce_scatter x1, waiting for transfers between devices: 47.3 us -> 40.8 us  [on_device(): lax.psum_scatter(-lax.dot_general(window, columns, (((0,), (1,)), ((), ()...]
    reduce_sum x0 -> x1, other arithmetic: none -> 6.51 us  [broadcast(): lax.all_gather(packet, axis_key).sum(axis=0)]
  transfers between devices with their start and end apart: 6 -> 6, of which waited for: 6 -> 6; matrix products, arithmetic and copies ran while one was open for 26% -> 25% of each run, Pallas kernels for 0% -> 0%
where the time goes in v1:
time: 353 us; the launch traced here: 352 us
  waiting for transfers between devices  223 us (63%)
  local copies, waits for them, and re-layouts  68.4 us (19%)
  matrix products  33.5 us (9%)
  between operations  14.2 us (4%)
  other arithmetic  12.8 us (4%)
    reduce_scatter x1, waiting for transfers between devices, on_device(): lax.psum_scatter(partial_value, 'row', scatter_dimension=1, tiled=True)  41.8 us
    reduce_scatter x1, waiting for transfers between devices, on_device(): lax.psum_scatter(-lax.dot_general(window, columns, (((0,), (1,)), ((), ()...  40.8 us
    all_gather x1, waiting for transfers between devices, broadcast(): lax.all_gather(packet, axis_key).sum(axis=0)  40.5 us
    all_gather x1, waiting for transfers between devices, on_device(): window = lax.all_gather(chosen, 'row', axis=1, tiled=True)  38.2 us
    reduce_scatter x1, waiting for transfers between devices, on_device(): lax.psum_scatter(crossed, 'row', scatter_dimension=0, tiled=True)  31 us
    all_gather x1, waiting for transfers between devices, on_device(): all_rows = lax.all_gather(normal, 'col', axis=0, tiled=True)  30.5 us
    gather x2, local copies, waits for them, and re-layouts, on_device(): jnp.take(ancestor_inverse.reshape(rows_here, range_blocks, BLK), local_id...  21.2 us
    unnamed x12, local copies, waits for them, and re-layouts  21.1 us
  transfers between devices with their start and end apart: 6, of which 6 were waited for; matrix products, arithmetic and copies ran while one was open for 25% of the time, Pallas kernels for 0%

profile of v1, /device:TPU:0, one launch (start us, length us, event | category | flops | bytes accessed | tf_op | source)
XLA Modules:
  0.0 352.0 jit_solution(10050021816249401080)
XLA Ops:
  7.2 0.0 copy-start
  7.2 0.0 copy-start.4
  7.2 0.0 reduce-scatter.4.cloned.1.call-start
  7.2 0.9 copy-done
  8.2 4.9 %fusion.16 = f32[1408,512]{0,1:T(8,128)} fusion(f32[1408,64]{0,1:T(8,128)S(1)} %copy-done, f32[64,512]{1,0:T(8,128)} %param.7), kind=kOutput, calls=%fused_computation.32 | convolution fusion | flops 553648128 | bytes 3375104 | tf_op jit(solution)/shard_map/dot_general | solution.py:31
  13.1 0.0 reduce-scatter.4.cloned.1.call-update
  13.1 0.0 all-gather.4.cloned.1.call-start
  13.2 41.8 %reduce-scatter.4.cloned.1.call-done = f32[1408,64]{0,1:T(8,128)} async-done(((f32[1408,512]{0,1:T(8,128)}), f32[1408,64]{0,1:T(8,128)}) %reduce-scatter.4.cloned.1.call-update) | async-done | bytes 360464 | tf_op jit(solution)/shard_map/reduce_scatter | solution.py:34
  54.9 0.0 all-gather.4.cloned.1.call-update
  55.0 0.0 all-gather.6.cloned.1.call-start
  55.0 0.0 copy-done.4
  55.0 0.1 copy.20
  55.1 0.1 reduce-window.8
  55.2 0.1 add_reduce_fusion
  55.3 30.5 %all-gather.4.cloned.1.call-done = f32[5632,64]{0,1:T(8,128)} async-done(((f32[1408,64]{0,1:T(8,128)}), f32[5632,64]{0,1:T(8,128)}) %all-gather.4.cloned.1.call-update) | async-done | bytes 1441808 | tf_op jit(solution)/shard_map/all_gather | solution.py:35
  85.8 1.5 reshape.103
  87.3 0.6 fusion.7
  87.9 0.9 copy.33
  88.8 0.0 all-gather.6.cloned.1.call-update
  88.8 0.0 all-gather.8.cloned.1.call-start
  88.9 0.1 convert_reduce_fusion
  89.0 38.2 %all-gather.6.cloned.1.call-done = f32[1536,512]{0,1:T(8,128)} async-done(((f32[1536,64]{0,1:T(8,128)}), f32[1536,512]{0,1:T(8,128)}) %all-gather.6.cloned.1.call-update) | async-done | bytes 3145744 | tf_op jit(solution)/shard_map/all_gather | solution.py:50
  127.2 2.4 copy.24
  129.6 4.0 %fusion.2 = f32[12,128,512]{2,0,1:T(8,128)S(1)} fusion(f32[12,128,512]{2,1,0:T(8,128)S(1)} %bitcast.36, pred[]{:T(512)S(6)} %eq.41, s32[12]{0:T(128)S(1)} %get-tuple-element.6, s32[12]{0:T(128)S(1)} %get-tuple-element.7), kind=kOutput, calls=%fused_computation.5 | convolution fusion | flops 114032784 | bytes 6291553 | tf_op jit(solution)/shard_map/kp,pbw->kbw/dot_general | solution.py:17
  133.6 3.4 copy.26
  137.1 0.0 all-gather.8.cloned.1.call-update
  137.1 0.0 reduce-scatter.6.cloned.1.call-start
  137.1 19.2 %copy.21 = f32[1536,3072]{0,1:T(8,128)} copy(f32[1536,3072]{1,0:T(8,128)} %param.5) | data formatting | bytes 37748736 | tf_op args[0]
  156.4 18.6 %copy.22 = f32[1536,24,128]{2,0,1:T(8,128)} copy(f32[1536,24,128]{0,2,1:T(8,128)} %bitcast.34) | data formatting | bytes 37748736 | tf_op jit(solution)/shard_map/reshape | solution.py:51
  175.0 11.2 %gather_fusion = f32[12,1536,128]{2,1,0:T(8,128)} fusion(f32[1536,24,128]{2,0,1:T(8,128)} %copy.22, s32[1024]{0:T(1024)S(1)} %pad_clamp_fusion), kind=kCustom, calls=%fused_computation | custom fusion | bytes 18874416 | tf_op jit(solution)/shard_map/jit(_take)/gather | solution.py:51
  186.3 9.9 %copy.23 = f32[1536,12,128]{0,2,1:T(8,128)} copy(f32[1536,12,128]{2,0,1:T(8,128)} %bitcast.35) | data formatting | bytes 18874368 | tf_op jit(solution)/shard_map/jit(_take)/gather | solution.py:51
  196.2 0.1 broadcast_bitcast_fusion
  196.3 0.0 copy-start.2
  196.3 4.5 %bitcast_select_fusion = f32[1536,1536]{0,1:T(8,128)S(1)} fusion(f32[1536,12,128]{0,2,1:T(8,128)} %copy.23, pred[1536]{0:T(1024)(128)(4,1)S(1)} %broadcast_bitcast_fusion), kind=kLoop, calls=%fused_computation.1 | loop fusion | flops 2359296 | bytes 18875904 | tf_op jit(solution)/shard_map/jit(_take)/select_n | solution.py:51
  200.8 0.0 copy-done.2
  200.8 17.1 %convolution_negate_fusion = f32[512,1536]{1,0:T(8,128)} fusion(f32[1536,512]{0,1:T(8,128)S(1)} %copy-done.2, f32[1536,1536]{0,1:T(8,128)S(1)} %bitcast_select_fusion), kind=kOutput, calls=%fused_computation.4 | convolution fusion | flops 14496301056 | bytes 15728640 | tf_op jit(solution)/shard_map/dot_general | solution.py:54
  217.9 0.0 reduce-scatter.6.cloned.1.call-update
  217.9 0.0 reduce-scatter.8.cloned.1.call-start
  218.0 40.5 %all-gather.8.cloned.1.call-done = f32[4,1536,512]{2,1,0:T(8,128)} async-done(((f32[1,1536,512]{2,1,0:T(8,128)}), f32[4,1536,512]{2,1,0:T(8,128)}) %all-gather.8.cloned.1.call-update) | async-done | bytes 12582928 | tf_op jit(solution)/shard_map/all_gather | solution.py:11
  258.5 6.5 %reduce_sum.29 = f32[1536,512]{1,0:T(8,128)S(1)} reduce(f32[4,1536,512]{2,1,0:T(8,128)} %all-gather.8.cloned.1.call-done, f32[]{:T(128)} %constant.52.clone.1), dimensions={0}, to_apply=%region_5.6 | reduce | flops 2359296 | bytes 15728644 | tf_op jit(solution)/shard_map/reduce_sum | solution.py:11
  265.1 0.0 copy-start.3
  265.1 40.8 %reduce-scatter.6.cloned.1.call-done = f32[128,1536]{1,0:T(8,128)} async-done(((f32[512,1536]{1,0:T(8,128)}), f32[128,1536]{1,0:T(8,128)}) %reduce-scatter.6.cloned.1.call-update) | async-done | bytes 786448 | tf_op jit(solution)/shard_map/reduce_scatter | solution.py:53
  305.9 6.9 %convolution_negate_fusion.1 = f32[512,128]{1,0:T(8,128)} fusion(f32[1536,512]{1,0:T(8,128)S(1)} %reduce_sum.29, f32[128,1536]{1,0:T(8,128)} %reduce-scatter.6.cloned.1.call-done), kind=kOutput, calls=%fused_computation.6 | convolution fusion | flops 1208025088 | bytes 4194304 | tf_op jit(solution)/shard_map/dot_general | solution.py:70
  312.7 0.0 reduce-scatter.8.cloned.1.call-update
  312.8 31.0 %reduce-scatter.8.cloned.1.call-done = f32[64,128]{1,0:T(8,128)} async-done(((f32[512,128]{1,0:T(8,128)}), f32[64,128]{1,0:T(8,128)}) %reduce-scatter.8.cloned.1.call-update) | async-done | bytes 32784 | tf_op jit(solution)/shard_map/reduce_scatter | solution.py:77
  343.8 0.0 copy-done.3
  343.8 1.4 add.49
  345.1 0.0 copy-done.1
  (6 shorter events, 0.0 us)
Async XLA Ops:
  7.2 1.0 copy-start
  7.2 47.8 %copy-start.4 = (s32[44]{0:T(128)S(1)}, s32[44]{0:T(128)}, u32[]{:S(2)}) copy-start(s32[44]{0:T(128)} %param.9) | copy-start | bytes 532
  7.2 47.8 %reduce-scatter.4.cloned.1.call-start = ((), (), s32[]{:S(2)}) async-start(), calls=%async_computation.3 | async-start | bytes 3244032 | tf_op jit(solution)/shard_map/reduce_scatter | solution.py:34
  13.1 72.7 %all-gather.4.cloned.1.call-start = ((), (), s32[]{:S(2)}) async-start(), calls=%async_computation.4 | async-start | bytes 1802240 | tf_op jit(solution)/shard_map/all_gather | solution.py:35
  55.0 72.2 %all-gather.6.cloned.1.call-start = ((), (), s32[]{:S(2)}) async-start(), calls=%async_computation.5 | async-start | bytes 3538944 | tf_op jit(solution)/shard_map/all_gather | solution.py:50
  88.8 169.7 %all-gather.8.cloned.1.call-start = ((), (), s32[]{:S(2)}) async-start(), calls=%async_computation.7 | async-start | bytes 15728640 | tf_op jit(solution)/shard_map/all_gather | solution.py:11
  137.1 168.8 %reduce-scatter.6.cloned.1.call-start = ((), (), s32[]{:S(2)}) async-start(), calls=%async_computation.6 | async-start | bytes 3932160 | tf_op jit(solution)/shard_map/reduce_scatter | solution.py:53
  196.3 4.6 %copy-start.2 = (f32[1536,512]{0,1:T(8,128)S(1)}, f32[1536,512]{0,1:T(8,128)}, u32[]{:S(2)}) copy-start(f32[1536,512]{0,1:T(8,128)} %all-gather.6.cloned.1.call-done) | copy-start | bytes 9437188
  217.9 125.8 %reduce-scatter.8.cloned.1.call-start = ((), (), s32[]{:S(2)}) async-start(), calls=%async_computation.8 | async-start | bytes 294912 | tf_op jit(solution)/shard_map/reduce_scatter | solution.py:77
  258.5 86.6 %copy-start.1 = (f32[1408,64]{0,1:T(8,128)S(1)}, f32[1408,64]{0,1:T(8,128)}, u32[]{:S(2)}) copy-start(f32[1408,64]{0,1:T(8,128)} %param.6) | copy-start | bytes 1081348
  265.1 78.7 %copy-start.3 = (f32[64,128]{1,0:T(8,128)S(1)}, f32[64,128]{1,0:T(8,128)}, u32[]{:S(2)}) copy-start(f32[64,128]{1,0:T(8,128)} %param.8) | copy-start | bytes 98308
Sparse Core Ops, SparseCore 0:
  13.2 41.6 reduce-scatter.3
  56.8 28.9 all-gather.3
  88.9 38.2 all-gather.5
  137.2 121.2 all-gather.7
  261.9 43.8 reduce-scatter.5
  312.9 30.8 reduce-scatter.7
